TPU v7x, 512 devices: a whole 4x4x16 slice. The times are simulated.
512 devices in a mesh: user: 32 (over z_hi, y, core), item: 16 (over x, z_lo).
Axes of the slice: x: 4, y: 4, z: 16 (z_hi: 4, z_lo: 4; z = z_hi * 4 + z_lo), core: 2. Of those that a mesh axis runs over, the one named last changes fastest.
Arguments:
- user_comps: bfloat16 [4096, 512], P(('user', 'item')), may hold values from -6 to 6
- item_text: bfloat16 [4096, 1024], P(('user', 'item')), may hold values from -6 to 6
- item_proj: bfloat16 [1024, 512], replicated, may hold values from -0.1875 to 0.1875
- w_in: float32 [64, 128], replicated, may hold values from -0.75 to 0.75
- b_in: float32 [128], replicated, may hold values from -4 to 4
- w_out: float32 [128, 64], replicated, may hold values from -1.5 to 1.5
- b_out: float32 [64], replicated, may hold values from -4 to 4
- pair_user: int32 [524288], P(('user', 'item')), may hold values from 0 to 127
- pair_item: int32 [524288], P(('user', 'item')), may hold values from 0 to 255
- teacher: float32 [524288], P(('user', 'item')), may hold values from -12 to 12
Outputs:
- user_grad: float32 [4096, 512], P(('user', 'item'))
- item_grad: float32 [4096, 512], P(('user', 'item'))
Inputs may be any that keep to these rules, and one draw needn't show every extreme that they name: `pair_user`: index of a user among the 128 users of the pair's tile. `pair_item`: index of an item among the 256 items of the pair's tile.
All inputs are finite; a program needn't handle non-finite values.
Results may differ from a plain program's by a relative error of at most 0.0058.
Values may be sent and summed in bfloat16 or wider, within the bound.
A program may use at most 64 MiB of HBM per device.

v0:
```python
import math

import jax
import jax.numpy as jnp
from jax import lax
from jax.sharding import PartitionSpec as P

COMPS = 8
CDIM = 64


gate_cap = 8.0


def copy_for_each(value, axis):
    count = lax.axis_size(axis)
    return lax.all_to_all(
        jnp.broadcast_to(value[None], (count, *value.shape)), axis, 0, 0, tiled=True
    )


def joined_along(pieces, dim):
    lengths = list(pieces.shape[1:])
    lengths[dim] *= pieces.shape[0]
    return jnp.moveaxis(pieces, 0, dim).reshape(lengths)


def gather_directly(value, axis, dim):
    pieces = copy_for_each(value, axis)
    return joined_along(pieces, dim)


def split_up(value, dim, count):
    lengths = value.shape
    pieces = value.reshape(*lengths[:dim], count, lengths[dim] // count, *lengths[dim + 1 :])
    return jnp.moveaxis(pieces, dim, 0)


def sent_and_summed(value, axis, dim):
    pieces = split_up(value, dim, lax.axis_size(axis))
    arrived = lax.all_to_all(pieces, axis, split_axis=0, concat_axis=0, tiled=True)
    return arrived.sum(axis=0)


def component_norm(values):
    mean_square = jnp.mean(values * values, axis=-1, keepdims=True)
    return values * lax.rsqrt(mean_square + 1e-06)


def project_rows(text_rows, projection):
    mixed = jnp.dot(text_rows, projection, preferred_element_type=jnp.float32)
    shaped = mixed.reshape(text_rows.shape[0], COMPS, CDIM)
    return component_norm(shaped).astype(jnp.bfloat16).reshape(text_rows.shape[0], COMPS * CDIM)


def spread_rows(onehot, values):
    upper = values.astype(jnp.bfloat16)
    lower = (values - upper.astype(jnp.float32)).astype(jnp.bfloat16)
    first = jnp.einsum("pr,pd->rd", onehot, upper, preferred_element_type=jnp.float32)
    return first + jnp.einsum("pr,pd->rd", onehot, lower, preferred_element_type=jnp.float32)


def item_terms(logit_gradient, user_portion):
    item_gradient = jnp.einsum(
        "uwx,uwz->uxz", logit_gradient, user_portion, preferred_element_type=jnp.float32
    )
    return item_gradient.reshape(item_gradient.shape[0], COMPS * CDIM)


def pair_grads(user_portion, item_portion, target, w_in, b_in, w_out, b_out, loss_scale):
    width = user_portion.shape[-1]
    reciprocal_norm = 1.0 / math.sqrt(width)
    mixture_logits = (
        jnp.einsum("xvw,xzw->xvz", user_portion, item_portion, preferred_element_type=jnp.float32)
        * reciprocal_norm
    )
    pair_count = mixture_logits.shape[0]
    flat_logits = mixture_logits.reshape(pair_count, -1)
    hidden_in = jnp.dot(flat_logits, w_in, precision=lax.Precision.HIGHEST) + b_in
    sig_pre = jax.nn.sigmoid(hidden_in)
    hidden = hidden_in * sig_pre
    gate_raw = jnp.dot(hidden, w_out, precision=lax.Precision.HIGHEST) + b_out
    capped = jnp.tanh(gate_raw / gate_cap)
    exp_gate = jnp.exp(gate_cap * capped)
    weights = exp_gate / jnp.sum(exp_gate, axis=-1, keepdims=True)
    student = jnp.sum(weights * flat_logits, axis=-1)
    residual_w = (student - target) * loss_scale
    d_gate = weights * (flat_logits - student[:, None]) * (1.0 - capped * capped)
    d_hidden = jnp.dot(d_gate, w_out.T, precision=lax.Precision.HIGHEST)
    d_pre = d_hidden * sig_pre * (1.0 + hidden_in * (1.0 - sig_pre))
    d_flat = residual_w[:, None] * (
        weights + jnp.dot(d_pre, w_in.T, precision=lax.Precision.HIGHEST)
    )
    logit_gradient = (d_flat * reciprocal_norm).astype(jnp.bfloat16).reshape(mixture_logits.shape)
    user_gradient = jnp.einsum(
        "ftz,fzr->ftr", logit_gradient, item_portion, preferred_element_type=jnp.float32
    )
    return (logit_gradient, user_gradient.reshape(pair_count, COMPS * CDIM))


def local(
    user_comps, item_text, item_proj, w_in, b_in, w_out, b_out, pair_user, pair_item, teacher
):
    user_tile = gather_directly(user_comps, "item", 0)
    item_tile = gather_directly(project_rows(item_text, item_proj), "user", 0)
    user_count = user_tile.shape[0]
    item_count = item_tile.shape[0]
    user_three = user_tile.reshape(user_count, COMPS, CDIM)
    item_three = item_tile.reshape(item_count, COMPS, CDIM)
    pair_total = pair_user.shape[0]
    block_rows = min(pair_total, 1024)
    block_total = pair_total // block_rows
    loss_scale = 2.0 * math.sqrt(user_count / (pair_total * lax.axis_size("item")))
    user_range = lax.iota(jnp.int32, user_count)
    item_range = lax.iota(jnp.int32, item_count)

    def one_block(step, carry):
        user_sum, item_sum, d_store = carry
        user_portion = jnp.take(user_three, pair_user, axis=0)
        item_portion = jnp.take(item_three, pair_item, axis=0)
        logit_gradient, user_gradient = pair_grads(
            user_portion, item_portion, teacher, w_in, b_in, w_out, b_out, loss_scale
        )
        user_onehot = (pair_user[:, None] == user_range[None, :]).astype(jnp.bfloat16)
        user_sum = user_sum + spread_rows(user_onehot, user_gradient)
        item_onehot = (pair_item[:, None] == item_range[None, :]).astype(jnp.bfloat16)
        item_sum = item_sum + spread_rows(item_onehot, item_terms(logit_gradient, user_portion))
        return (user_sum, item_sum, d_store)

    item_start = jnp.zeros((item_count, COMPS * CDIM), jnp.float32)
    store_start = jnp.zeros((1, COMPS, COMPS), jnp.bfloat16)
    start_carry = (jnp.zeros((user_count, COMPS * CDIM), jnp.float32), item_start, store_start)
    grad_users, grad_items, d_store = lax.fori_loop(0, block_total, one_block, start_carry)
    user_grad = sent_and_summed(grad_users, "item", 0)
    item_grad = sent_and_summed(grad_items, "user", 0)
    return (user_grad, item_grad)


def solution(mesh):
    in_specs = (
        P(("user", "item"), None),
        P(("user", "item"), None),
        P(),
        P(),
        P(),
        P(),
        P(),
        P(("user", "item")),
        P(("user", "item")),
        P(("user", "item")),
    )
    out_specs = (P(("user", "item"), None), P(("user", "item"), None))
    return jax.shard_map(local, mesh=mesh, in_specs=in_specs, out_specs=out_specs, check_vma=False)
```

profile of v0, /device:TPU:22, one launch (start us, length us, event | category | flops | bytes accessed | tf_op | source)
XLA Modules:
  0.0 155.3 jit_solution(1507555423901665601)
XLA Ops:
  0.7 1.4 broadcast_in_dim.60
  2.1 8.9 %all-to-all-start = ((bf16[16,8,512]{2,1,0:T(8,128)(2,1)}), bf16[16,8,512]{2,1,0:T(8,128)(2,1)S(1)}, u32[]{:S(2)}, u32[]{:S(2)}) async-start(bf16[16,8,512]{2,1,0:T(8,128)(2,1)} %broadcast_in_dim.60), calls=%async_computation | async-start | bytes 262144 | tf_op jit(solution)/shard_map/all_to_all | solution.py:17
  11.0 1.0 fusion.47
  12.3 5.1 %all-to-all-done = bf16[16,8,512]{2,1,0:T(8,128)(2,1)S(1)} async-done(((bf16[16,8,512]{2,1,0:T(8,128)(2,1)}), bf16[16,8,512]{2,1,0:T(8,128)(2,1)S(1)}, u32[]{:S(2)}, u32[]{:S(2)}) %all-to-all-start) | async-done | bytes 131104 | tf_op jit(solution)/shard_map/all_to_all | solution.py:17
  18.1 15.6 %all-to-all-start.1 = ((bf16[32,8,512]{2,1,0:T(8,128)(2,1)}), bf16[32,8,512]{2,1,0:T(8,128)(2,1)}, u32[]{:S(2)}, u32[]{:S(2)}) async-start(bf16[32,8,512]{2,1,0:T(8,128)(2,1)} %broadcast_in_dim.64), calls=%async_computation.1 | async-start | bytes 524288 | tf_op jit(solution)/shard_map/all_to_all | solution.py:17
  33.9 3.3 %gather_fusion = bf16[1024,8,64]{2,1,0:T(8,128)(2,1)S(1)} fusion(bf16[128,8,64]{2,1,0:T(8,128)(2,1)S(1)} %reshape_reshape.6, s32[1024]{0:T(1024)S(1)} %fusion.39), kind=kCustom, calls=%fused_computation | custom fusion | bytes 2101248 | tf_op jit(solution)/shard_map/while/body/eval_jaxpr/jit(_take)/gather | solution.py:119
  37.3 15.3 %all-to-all-done.1 = bf16[32,8,512]{2,1,0:T(8,128)(2,1)} async-done(((bf16[32,8,512]{2,1,0:T(8,128)(2,1)}), bf16[32,8,512]{2,1,0:T(8,128)(2,1)}, u32[]{:S(2)}, u32[]{:S(2)}) %all-to-all-start.1) | async-done | bytes 262176 | tf_op jit(solution)/shard_map/all_to_all | solution.py:17
  52.5 2.1 %reshape_reshape.7 = bf16[256,8,64]{2,1,0:T(8,128)(2,1)} reshape(bf16[32,8,512]{2,1,0:T(8,128)(2,1)} %all-to-all-done.1) | data formatting | bytes 524288 | tf_op jit(solution)/shard_map/reshape;reshape | solution.py:109
  54.6 8.7 %gather_fusion.1 = bf16[1024,8,64]{2,1,0:T(8,128)(2,1)} fusion(bf16[256,8,64]{2,1,0:T(8,128)(2,1)} %reshape_reshape.7, s32[1024]{0:T(1024)S(1)} %fusion.40), kind=kCustom, calls=%fused_computation.1 | custom fusion | bytes 2101248 | tf_op jit(solution)/shard_map/while/body/eval_jaxpr/jit(_take)/gather | solution.py:120
  63.3 7.7 %convolution_multiply_fusion = f32[1024,8,8]{2,1,0:T(8,128)} fusion(bf16[1024,8,64]{2,1,0:T(8,128)(2,1)S(1)} %gather_fusion, pred[1024]{0:T(1024)(128)(4,1)S(1)} %get-tuple-element.39, bf16[1024,8,64]{2,1,0:T(8,128)(2,1)} %gather_fusion.1, pred[1024]{0:T(1024)(128)(4,1)S(1)} %get-tuple-element.38), kind=kOutput, calls=%fused_computation.2 | convolution fusion | flops 9502720 | bytes 2361344 | tf_op jit(solution)/shard_map/while/body/eval_jaxpr/xvw,xzw->xvz/dot_general | solution.py:74
  71.0 2.8 %copy.16 = f32[1024,8,8]{0,2,1:T(8,128)S(1)} copy(f32[1024,8,8]{2,1,0:T(8,128)} %convolution_multiply_fusion) | data formatting | bytes 524288 | tf_op jit(solution)/shard_map/while/body/eval_jaxpr/mul | solution.py:74
  73.8 1.0 convolution_add_fusion.1
  75.8 1.0 fusion.3
  77.6 2.4 %copy.19 = bf16[1024,8,8]{1,2,0:T(8,128)(2,1)} copy(bf16[1024,8,8]{0,2,1:T(8,128)(2,1)S(1)} %fusion.10) | data formatting | bytes 262144 | tf_op jit(solution)/shard_map/while/body/eval_jaxpr/reshape | solution.py:94
  80.0 7.0 %fusion.13 = f32[1024,8,64]{2,1,0:T(8,128)} fusion(bf16[1024,8,8]{1,2,0:T(8,128)(2,1)} %copy.19, bf16[1024,8,64]{2,1,0:T(8,128)(2,1)} %gather_fusion.1, pred[1024]{0:T(1024)(128)(4,1)S(1)} %get-tuple-element.38), kind=kOutput, calls=%fused_computation.29 | convolution fusion | flops 8912896 | bytes 3277824 | tf_op jit(solution)/shard_map/while/body/eval_jaxpr/ftz,fzr->ftr/dot_general | solution.py:95
  87.0 3.8 %copy.18 = f32[1024,8,64]{0,2,1:T(8,128)} copy(f32[1024,8,64]{2,1,0:T(8,128)} %fusion.13) | data formatting | bytes 4194304 | tf_op jit(solution)/shard_map/while/body/eval_jaxpr/ftz,fzr->ftr/dot_general | solution.py:95
  90.8 2.0 %fusion.1 = (bf16[1024,512]{0,1:T(8,128)(2,1)S(1)}, bf16[1024,512]{0,1:T(8,128)(2,1)S(1)}) fusion(f32[1024,8,64]{0,2,1:T(8,128)} %copy.18), kind=kLoop, calls=%fused_computation.8 | loop fusion | flops 2097152 | bytes 4194304 | tf_op jit(solution)/shard_map/while/body/eval_jaxpr/convert_element_type | solution.py:58
  93.5 1.4 fusion.8
  95.0 8.2 %all-to-all-start.2 = ((f32[16,8,512]{2,1,0:T(8,128)}), f32[16,8,512]{2,1,0:T(8,128)S(1)}, u32[]{:S(2)}, u32[]{:S(2)}) async-start(f32[16,8,512]{2,1,0:T(8,128)} %fusion.8), calls=%async_computation.2 | async-start | bytes 524288 | tf_op jit(solution)/shard_map/all_to_all | solution.py:41
  103.1 6.4 %fusion.12 = f32[1024,8,64]{2,1,0:T(8,128)} fusion(bf16[1024,8,8]{1,2,0:T(8,128)(2,1)} %copy.19, bf16[1024,8,64]{2,1,0:T(8,128)(2,1)S(1)} %gather_fusion, pred[1024]{0:T(1024)(128)(4,1)S(1)} %get-tuple-element.39), kind=kOutput, calls=%fused_computation.28 | convolution fusion | flops 8912896 | bytes 3277824 | tf_op jit(solution)/shard_map/while/body/eval_jaxpr/uwx,uwz->uxz/dot_general | solution.py:64
  109.5 2.8 %copy.20 = f32[1024,8,64]{0,2,1:T(8,128)S(1)} copy(f32[1024,8,64]{2,1,0:T(8,128)} %fusion.12) | data formatting | bytes 4194304 | tf_op jit(solution)/shard_map/while/body/eval_jaxpr/uwx,uwz->uxz/dot_general | solution.py:64
  113.4 1.5 fusion.2
  114.9 6.1 %all-to-all-start.3 = ((f32[32,8,512]{2,1,0:T(8,128)}), f32[32,8,512]{2,1,0:T(8,128)S(1)}, u32[]{:S(2)}, u32[]{:S(2)}) async-start(f32[32,8,512]{2,1,0:T(8,128)} %fusion.2), calls=%async_computation.3 | async-start | bytes 1048576 | tf_op jit(solution)/shard_map/all_to_all | solution.py:41
  121.6 33.1 %all-to-all-done.3 = f32[32,8,512]{2,1,0:T(8,128)S(1)} async-done(((f32[32,8,512]{2,1,0:T(8,128)}), f32[32,8,512]{2,1,0:T(8,128)S(1)}, u32[]{:S(2)}, u32[]{:S(2)}) %all-to-all-start.3) | async-done | bytes 524320 | tf_op jit(solution)/shard_map/all_to_all | solution.py:41
  (37 shorter events, 6.0 us)
Async XLA Ops:
  0.6 10.3 %copy-start = (bf16[1024,512]{1,0:T(8,128)(2,1)S(1)}, bf16[1024,512]{1,0:T(8,128)(2,1)}, u32[]{:S(2)}) copy-start(bf16[1024,512]{1,0:T(8,128)(2,1)} %param.12) | copy-start | bytes 3145732
  0.6 33.0 %copy-start.1 = (s32[1024]{0:T(1024)S(1)}, s32[1024]{0:T(1024)}, u32[]{:S(2)}) copy-start(s32[1024]{0:T(1024)} %param.17) | copy-start | bytes 12292
  0.7 33.1 %copy-start.2 = (s32[1024]{0:T(1024)S(1)}, s32[1024]{0:T(1024)}, u32[]{:S(2)}) copy-start(s32[1024]{0:T(1024)} %param.18) | copy-start | bytes 12292
  2.1 15.3 %all-to-all-start = ((bf16[16,8,512]{2,1,0:T(8,128)(2,1)}), bf16[16,8,512]{2,1,0:T(8,128)(2,1)S(1)}, u32[]{:S(2)}, u32[]{:S(2)}) async-start(bf16[16,8,512]{2,1,0:T(8,128)(2,1)} %broadcast_in_dim.60), calls=%async_computation | async-start | bytes 262144 | tf_op jit(solution)/shard_map/all_to_all | solution.py:17
  18.1 34.4 %all-to-all-start.1 = ((bf16[32,8,512]{2,1,0:T(8,128)(2,1)}), bf16[32,8,512]{2,1,0:T(8,128)(2,1)}, u32[]{:S(2)}, u32[]{:S(2)}) async-start(bf16[32,8,512]{2,1,0:T(8,128)(2,1)} %broadcast_in_dim.64), calls=%async_computation.1 | async-start | bytes 524288 | tf_op jit(solution)/shard_map/all_to_all | solution.py:17
  71.0 2.9 %copy-start.3 = (f32[64,128]{1,0:T(8,128)S(1)}, f32[64,128]{1,0:T(8,128)}, u32[]{:S(2)}) copy-start(f32[64,128]{1,0:T(8,128)} %param.13) | copy-start | bytes 98308
  71.0 2.9 %copy-start.5 = (f32[128]{0:T(128)S(1)}, f32[128]{0:T(128)}, u32[]{:S(2)}) copy-start(f32[128]{0:T(128)} %param.14) | copy-start | bytes 1540
  71.0 3.9 %copy-start.6 = (f32[128,64]{0,1:T(8,128)S(1)}, f32[128,64]{0,1:T(8,128)}, u32[]{:S(2)}) copy-start(f32[128,64]{0,1:T(8,128)} %param.15) | copy-start | bytes 98308
  71.0 3.9 %copy-start.7 = (f32[64]{0:T(128)S(1)}, f32[64]{0:T(128)}, u32[]{:S(2)}) copy-start(f32[64]{0:T(128)} %param.16) | copy-start | bytes 772
  75.8 1.0 copy-start.4
  95.0 19.9 %all-to-all-start.2 = ((f32[16,8,512]{2,1,0:T(8,128)}), f32[16,8,512]{2,1,0:T(8,128)S(1)}, u32[]{:S(2)}, u32[]{:S(2)}) async-start(f32[16,8,512]{2,1,0:T(8,128)} %fusion.8), calls=%async_computation.2 | async-start | bytes 524288 | tf_op jit(solution)/shard_map/all_to_all | solution.py:41
  114.9 39.8 %all-to-all-start.3 = ((f32[32,8,512]{2,1,0:T(8,128)}), f32[32,8,512]{2,1,0:T(8,128)S(1)}, u32[]{:S(2)}, u32[]{:S(2)}) async-start(f32[32,8,512]{2,1,0:T(8,128)} %fusion.2), calls=%async_computation.3 | async-start | bytes 1048576 | tf_op jit(solution)/shard_map/all_to_all | solution.py:41
where the time goes:
time: 156 us; the launch traced here: 155 us
  waiting for transfers between devices  53.5 us (34%)
  starting transfers between devices  38.6 us (25%)
  matrix products  30 us (19%)
  local copies, waits for them, and re-layouts  28.6 us (18%)
  other arithmetic  3.76 us (2%)
    all_to_all x2, waiting for transfers between devices, sent_and_summed(): lax.all_to_all(pieces, axis, split_axis=0, concat_axis=0, tiled=True)  33.1 us
    all_to_all x2, starting transfers between devices, copy_for_each(): lax.all_to_all(jnp.broadcast_to(value[None], (count, *value.shape)), axis...  24.4 us
    all_to_all x2, waiting for transfers between devices, copy_for_each(): lax.all_to_all(jnp.broadcast_to(value[None], (count, *value.shape)), axis...  20.4 us
    all_to_all x2, starting transfers between devices, sent_and_summed(): lax.all_to_all(pieces, axis, split_axis=0, concat_axis=0, tiled=True)  14.2 us
    gather x1, local copies, waits for them, and re-layouts, one_block(): item_portion = jnp.take(item_three, pair_item, axis=0)  8.69 us
    dot_general x1, matrix products, pair_grads(): jnp.einsum('xvw,xzw->xvz', user_portion, item_portion, preferred_element_...  7.68 us
    dot_general x1, matrix products, pair_grads(): jnp.einsum('ftz,fzr->ftr', logit_gradient, item_portion, preferred_elemen...  7.02 us
    dot_general x1, matrix products, item_terms(): jnp.einsum('uwx,uwz->uxz', logit_gradient, user_portion, preferred_elemen...  6.4 us
  transfers between devices with their start and end apart: 4, of which 3 were waited for; matrix products, arithmetic and copies ran while one was open for 11% of the time, Pallas kernels for 0%

commit v1 on v0

v1 whole, which is shorter than its diff:
```python
import math

import jax
import jax.numpy as jnp
from jax import lax
from jax.experimental import pallas as pl
from jax.experimental.pallas import tpu as pltpu
from jax.sharding import PartitionSpec as P

MESH = pl.DeviceIdType.MESH
BF16 = jnp.bfloat16
F32 = jnp.float32

COMPS = 8
CDIM = 64
WIDE = COMPS * CDIM
GATES = 64
HIDDEN = 128
ROWS = 8
N_USER = 32
N_ITEM = 16
N_Z = 4
N_YC = 8
USERS = ROWS * N_ITEM
ITEMS = ROWS * N_USER
PAIRS = 1024
LANES = 128
CHUNKS = PAIRS // LANES
LOSS_SCALE = 2.0 * math.sqrt(USERS / (PAIRS * N_ITEM))
NT = (((1,), (1,)), ((), ()))
TN = (((0,), (0,)), ((), ()))


def dot(a, b, dims=(((1,), (0,)), ((), ()))):
    return lax.dot_general(a, b, dims, preferred_element_type=F32)


def split(x):
    upper = x.astype(BF16)
    return upper, (x - upper.astype(F32)).astype(BF16)


def store_parts(ref, x, lanes):
    n = x.shape[0]
    upper, lower = split(x)
    ref[0:n, lanes] = upper
    ref[n : 2 * n, lanes] = lower
    ref[2 * n : 3 * n, lanes] = upper


def chunk(g):
    return slice(g * LANES, (g + 1) * LANES)


def moving(g):
    return pl.ds(pl.multiple_of(g * LANES, LANES), LANES)


def kernel(
    uc_h, it_h, ip_h, win_h, bin_h, wout_h, bout_h, pu_h, pi_h, te_h,
    ug_o, ig_o,
    uc, it, ip, win, bin_, wout, bout, pu, pi, te,
    ubuf, ibuf, wot, bot, bcol, bocol, w1, w2, w3, w4,
    ohu, ohi, up, un, vn, logits, x1, x2, x3, x4, pre_r, sil_r, raw_r, wt_r, res_r, grad_r,
    igt, ugt, isum, usum, asend, abuf, bsend, bbuf, csend, cbuf,
    in_sem, zs, ys, us, isem, usem, as_, asem, bs, bsem, cs, csem,
):
    me_u = lax.axis_index("user")
    me_i = lax.axis_index("item")
    z = me_u // N_YC
    yc = me_u % N_YC

    barrier = pltpu.get_barrier_semaphore()

    def greet(a, b):
        pl.semaphore_signal(barrier, inc=1, device_id=(a, b), device_id_type=MESH)

    for o in (2, 1, 3):
        greet((z + o) % N_Z * N_YC + yc, me_i)
    for o in range(1, N_YC):
        greet(z * N_YC + (yc + o) % N_YC, me_i)
    for o in range(1, N_ITEM):
        greet(me_u, (me_i + o) % N_ITEM)

    pairs_in = [
        (ip_h, ip), (it_h, it), (uc_h, uc), (win_h, win), (bin_h, bin_), (wout_h, wout),
        (bout_h, bout), (pu_h, pu), (pi_h, pi), (te_h, te),
    ]
    loads = [pltpu.make_async_copy(s, d, in_sem.at[n]) for n, (s, d) in enumerate(pairs_in)]
    for load in loads:
        load.start()

    row = lax.broadcasted_iota(jnp.int32, (WIDE, WIDE), 0)
    col = lax.broadcasted_iota(jnp.int32, (WIDE, WIDE), 1)
    blocks = jnp.where(row // CDIM == col // CDIM, 1.0, 0.0).astype(BF16)
    loads[0].wait()
    loads[1].wait()
    mixed = dot(it[...], ip[...])
    upper, lower = split(mixed * mixed)
    square = dot(upper, blocks) + dot(lower, blocks)
    own_item = mixed * lax.rsqrt(square * (1.0 / CDIM) + 1e-06)
    ibuf[me_u] = own_item.astype(BF16)
    loads[2].wait()
    ubuf[me_i] = uc[...]

    pl.semaphore_wait(barrier, (N_Z - 1) + (N_YC - 1) + (N_ITEM - 1))

    def item_send(slot, peer, sem):
        return pltpu.make_async_remote_copy(
            src_ref=ibuf.at[slot], dst_ref=ibuf.at[slot], send_sem=sem, recv_sem=isem.at[slot],
            device_id=(peer, me_i), device_id_type=MESH,
        )

    sends = []
    for n, o in enumerate((2, 1, 3)):
        copy = item_send(me_u, (z + o) % N_Z * N_YC + yc, zs.at[n])
        copy.start()
        sends.append(copy)

    def pass_on(o):
        slot = (z + o) % N_Z * N_YC + yc
        for q in range(1, N_YC):
            copy = item_send(slot, z * N_YC + (yc + q) % N_YC, ys.at[o * N_YC + q])
            copy.start()
            sends.append(copy)

    pass_on(0)

    def user_send(slot, peer, sem):
        return pltpu.make_async_remote_copy(
            src_ref=ubuf.at[slot], dst_ref=ubuf.at[slot], send_sem=sem, recv_sem=usem.at[slot],
            device_id=(me_u, peer), device_id_type=MESH,
        )

    for o in range(1, N_ITEM):
        copy = user_send(me_i, (me_i + o) % N_ITEM, us.at[o])
        copy.start()
        sends.append(copy)

    for o in (1, 3):
        slot = (z + o) % N_Z * N_YC + yc
        item_send(slot, me_u, zs.at[0]).wait_recv()
        pass_on(o)

    for load in loads[3:]:
        load.wait()
    wot[...] = jnp.transpose(wout[...])
    bot[...] = jnp.transpose(jnp.broadcast_to(bout[...], (LANES, GATES)))
    bcol[...] = jnp.transpose(jnp.broadcast_to(bin_[...], (LANES, HIDDEN)))

    def reordered(ref):
        return jnp.concatenate([ref[pl.ds(k, COMPS, stride=COMPS), :] for k in range(COMPS)], axis=0)

    bocol[...] = reordered(bot)
    zeros = jnp.zeros((GATES, HIDDEN), F32)
    for source, tall, flat in ((win, w1, w4), (wot, w3, w2)):
        w = reordered(source)
        upper, lower = split(w)
        flat[:, 0:HIDDEN] = upper
        flat[:, HIDDEN : 2 * HIDDEN] = upper
        flat[:, 2 * HIDDEN : 3 * HIDDEN] = lower
        upper, lower = upper.astype(F32), lower.astype(F32)
        stacked = jnp.concatenate([upper, upper, lower, zeros], axis=0)
        tall[...] = jnp.transpose(stacked).astype(BF16)

    user_range = lax.broadcasted_iota(jnp.int32, (USERS, LANES), 0)
    item_range = lax.broadcasted_iota(jnp.int32, (ITEMS, LANES), 0)
    for g in range(CHUNKS):
        ohu[:, chunk(g)] = jnp.where(user_range == pu[g : g + 1, :], 1.0, 0.0).astype(BF16)
        ohi[:, chunk(g)] = jnp.where(item_range == pi[g : g + 1, :], 1.0, 0.0).astype(BF16)
    x1[3 * GATES :, :] = jnp.zeros((GATES, PAIRS), BF16)
    x3[3 * GATES :, :] = jnp.zeros((GATES, PAIRS), BF16)
    shuffle = jnp.where(col == row % CDIM * COMPS + row // CDIM, 1.0, 0.0).astype(BF16)

    slot = (z + 2) % N_Z * N_YC + yc
    item_send(slot, me_u, zs.at[0]).wait_recv()
    pass_on(2)

    for o in range(1, N_ITEM):
        user_send((me_i + o) % N_ITEM, me_i, us.at[0]).wait_recv()
    user_tile = ubuf[...].astype(F32).reshape(USERS, WIDE).astype(BF16)
    un[...] = dot(user_tile, ohu[...], TN)
    up[...] = dot(dot(user_tile, shuffle).astype(BF16), ohu[...], TN)

    for o in range(N_Z):
        for q in range(1, N_YC):
            item_send((z + o) % N_Z * N_YC + (yc + q) % N_YC, me_u, zs.at[0]).wait_recv()
    item_tile = ibuf[...].astype(F32).reshape(ITEMS, WIDE).astype(BF16)
    vn[...] = dot(item_tile, ohi[...], TN).reshape(vn.shape)

    def logit_chunk(g, _):
        lanes = moving(g)

        def step(block, total):
            total = list(total)
            for j in range(8):
                d = block * 8 + j
                u = up[pl.ds(pl.multiple_of(d * COMPS, COMPS), COMPS), lanes]
                for k in range(COMPS):
                    total[k] = total[k] + u * vn[k * 8 + block, j : j + 1, lanes]
            return tuple(total)

        total = lax.fori_loop(0, CDIM // 8, step, (jnp.zeros((COMPS, LANES), F32),) * COMPS)
        x = jnp.concatenate(total, axis=0) * (1.0 / math.sqrt(CDIM))
        logits[:, lanes] = x
        store_parts(x1, x, lanes)
        return 0

    lax.fori_loop(0, CHUNKS, logit_chunk, 0)

    pre_r[...] = dot(w1[...], x1[...])
    for g in range(CHUNKS):
        pre = pre_r[:, chunk(g)] + bcol[...]
        sig = 0.5 * jnp.tanh(0.5 * pre) + 0.5
        store_parts(x2, pre * sig, chunk(g))
        sil_r[:, chunk(g)] = sig * (1.0 + pre * (1.0 - sig))
    raw_r[...] = dot(w2[...], x2[...])
    for g in range(CHUNKS):
        capped = jnp.tanh((raw_r[:, chunk(g)] + bocol[...]) * 0.125)
        powers = jnp.exp(8.0 * capped)
        weights = powers * (1.0 / jnp.sum(powers, axis=0, keepdims=True))
        flat = logits[:, chunk(g)]
        student = jnp.sum(weights * flat, axis=0, keepdims=True)
        store_parts(x3, weights * (flat - student) * (1.0 - capped * capped), chunk(g))
        wt_r[:, chunk(g)] = weights
        res_r[g : g + 1, :] = (student - te[g : g + 1, :]) * LOSS_SCALE
    pre_r[...] = dot(w3[...], x3[...])
    for g in range(CHUNKS):
        store_parts(x4, pre_r[:, chunk(g)] * sil_r[:, chunk(g)], chunk(g))
    raw_r[...] = dot(w4[...], x4[...])
    for g in range(CHUNKS):
        d_flat = res_r[g : g + 1, :] * (wt_r[:, chunk(g)] + raw_r[:, chunk(g)])
        grad_r[:, chunk(g)] = (d_flat * (1.0 / math.sqrt(CDIM))).astype(BF16).astype(F32)

    def item_chunk(g, _):
        lanes = moving(g)
        for k in range(COMPS):
            total = None
            for c in range(COMPS):
                term = grad_r[k * COMPS + c : k * COMPS + c + 1, lanes] * un[c * CDIM : (c + 1) * CDIM, lanes]
                total = term if total is None else total + term
            igt[k * CDIM : (k + 1) * CDIM, lanes] = total.astype(BF16)
        return 0

    lax.fori_loop(0, CHUNKS, item_chunk, 0)
    isum[...] = dot(ohi[...], igt[...], NT).reshape(N_Z, N_YC, ROWS, WIDE)
    asend[...] = isum[...].astype(BF16)

    for o in range(1, N_YC):
        peer = (yc + o) % N_YC
        copy = pltpu.make_async_remote_copy(
            src_ref=asend.at[:, peer], dst_ref=abuf.at[yc], send_sem=as_.at[o], recv_sem=asem.at[yc],
            device_id=(z * N_YC + peer, me_i), device_id_type=MESH,
        )
        copy.start()
        sends.append(copy)

    def user_chunk(g, _):
        lanes = moving(g)
        for c in range(COMPS):
            total = None
            for k in range(COMPS):
                term = grad_r[k * COMPS + c : k * COMPS + c + 1, lanes] * vn[k * 8 : (k + 1) * 8, :, lanes].reshape(CDIM, LANES)
                total = term if total is None else total + term
            ugt[c * CDIM : (c + 1) * CDIM, lanes] = total.astype(BF16)
        return 0

    lax.fori_loop(0, CHUNKS, user_chunk, 0)
    usum[...] = dot(ohu[...], ugt[...], NT).reshape(N_ITEM, ROWS, WIDE)
    csend[...] = usum[...].astype(BF16)
    for o in range(1, N_ITEM):
        peer = (me_i + o) % N_ITEM
        copy = pltpu.make_async_remote_copy(
            src_ref=csend.at[peer], dst_ref=cbuf.at[me_i], send_sem=cs.at[o], recv_sem=csem.at[me_i],
            device_id=(me_u, peer), device_id_type=MESH,
        )
        copy.start()
        sends.append(copy)

    partial = isum[:, yc]
    for o in range(1, N_YC):
        peer = (yc + o) % N_YC
        pltpu.make_async_remote_copy(
            src_ref=abuf.at[peer], dst_ref=abuf.at[peer], send_sem=as_.at[0], recv_sem=asem.at[peer],
            device_id=(me_u, me_i), device_id_type=MESH,
        ).wait_recv()
        partial = partial + abuf[peer].astype(F32)
    bsend[...] = partial.astype(BF16)
    isum[:, 0] = partial
    for n, o in enumerate((2, 1, 3)):
        peer = (z + o) % N_Z
        copy = pltpu.make_async_remote_copy(
            src_ref=bsend.at[peer], dst_ref=bbuf.at[z], send_sem=bs.at[n], recv_sem=bsem.at[z],
            device_id=(peer * N_YC + yc, me_i), device_id_type=MESH,
        )
        copy.start()
        sends.append(copy)

    total = usum[me_i]
    for o in range(1, N_ITEM):
        peer = (me_i + o) % N_ITEM
        pltpu.make_async_remote_copy(
            src_ref=cbuf.at[peer], dst_ref=cbuf.at[peer], send_sem=cs.at[0], recv_sem=csem.at[peer],
            device_id=(me_u, me_i), device_id_type=MESH,
        ).wait_recv()
        total = total + cbuf[peer].astype(F32)
    ug_o[...] = total

    total = isum[z, 0]
    for o in (1, 3, 2):
        peer = (z + o) % N_Z
        pltpu.make_async_remote_copy(
            src_ref=bbuf.at[peer], dst_ref=bbuf.at[peer], send_sem=bs.at[0], recv_sem=bsem.at[peer],
            device_id=(me_u, me_i), device_id_type=MESH,
        ).wait_recv()
        total = total + bbuf[peer].astype(F32)
    ig_o[...] = total

    for copy in sends:
        copy.wait_send()


def local(
    user_comps, item_text, item_proj, w_in, b_in, w_out, b_out, pair_user, pair_item, teacher
):
    def vmem(shape, kind=F32):
        return pltpu.VMEM(shape, kind)

    inputs = (
        user_comps, item_text, item_proj, w_in, b_in.reshape(1, -1), w_out, b_out.reshape(1, -1),
        pair_user.reshape(CHUNKS, LANES), pair_item.reshape(CHUNKS, LANES), teacher.reshape(CHUNKS, LANES),
    )
    dma = pltpu.SemaphoreType.DMA
    scratch = [vmem(a.shape, a.dtype) for a in inputs] + [
        vmem((N_ITEM, ROWS, WIDE), BF16),
        vmem((N_USER, ROWS, WIDE), BF16),
        vmem((GATES, HIDDEN)),
        vmem((GATES, LANES)),
        vmem((HIDDEN, LANES)),
        vmem((GATES, LANES)),
        vmem((HIDDEN, 4 * GATES), BF16),
        vmem((GATES, 3 * HIDDEN), BF16),
        vmem((HIDDEN, 4 * GATES), BF16),
        vmem((GATES, 3 * HIDDEN), BF16),
        vmem((USERS, PAIRS), BF16),
        vmem((ITEMS, PAIRS), BF16),
        vmem((WIDE, PAIRS)),
        vmem((WIDE, PAIRS)),
        vmem((WIDE // 8, 8, PAIRS)),
        vmem((GATES, PAIRS)),
        vmem((4 * GATES, PAIRS), BF16),
        vmem((3 * HIDDEN, PAIRS), BF16),
        vmem((4 * GATES, PAIRS), BF16),
        vmem((3 * HIDDEN, PAIRS), BF16),
        vmem((HIDDEN, PAIRS)),
        vmem((HIDDEN, PAIRS)),
        vmem((GATES, PAIRS)),
        vmem((GATES, PAIRS)),
        vmem((CHUNKS, LANES)),
        vmem((GATES, PAIRS)),
        vmem((WIDE, PAIRS), BF16),
        vmem((WIDE, PAIRS), BF16),
        vmem((N_Z, N_YC, ROWS, WIDE)),
        vmem((N_ITEM, ROWS, WIDE)),
        vmem((N_Z, N_YC, ROWS, WIDE), BF16),
        vmem((N_YC, N_Z, ROWS, WIDE), BF16),
        vmem((N_Z, ROWS, WIDE), BF16),
        vmem((N_Z, ROWS, WIDE), BF16),
        vmem((N_ITEM, ROWS, WIDE), BF16),
        vmem((N_ITEM, ROWS, WIDE), BF16),
        dma((len(inputs),)),
        dma((N_Z,)),
        dma((N_Z * N_YC,)),
        dma((N_ITEM,)),
        dma((N_USER,)),
        dma((N_ITEM,)),
        dma((N_YC,)),
        dma((N_YC,)),
        dma((N_Z,)),
        dma((N_Z,)),
        dma((N_ITEM,)),
        dma((N_ITEM,)),
    ]
    out = jax.ShapeDtypeStruct((ROWS, WIDE), F32)
    return pl.pallas_call(
        kernel,
        out_shape=(out, out),
        in_specs=[pl.BlockSpec(memory_space=pl.ANY)] * len(inputs),
        out_specs=(pl.BlockSpec(memory_space=pltpu.VMEM),) * 2,
        scratch_shapes=scratch,
        compiler_params=pltpu.CompilerParams(
            collective_id=0, has_side_effects=True, vmem_limit_bytes=60 * 1024 * 1024
        ),
    )(*inputs)


def solution(mesh):
    split_both = P(("user", "item"), None)
    split_one = P(("user", "item"))
    in_specs = (
        split_both, split_both, P(), P(), P(), P(), P(), split_one, split_one, split_one,
    )
    return jax.shard_map(
        local, mesh=mesh, in_specs=in_specs, out_specs=(split_both, split_both), check_vma=False
    )
```

time: 156 us -> 50.9 us (0.33)
  the two profiles are of different devices: /device:TPU:22 before, /device:TPU:1 now
where the time goes in v1:
time: 50.9 us; the launch traced here: 50.6 us
  Pallas kernels  46.5 us (91%)
  local copies, waits for them, and re-layouts  3.41 us (7%)
  between operations  0.65 us (1%)
    pallas_call x1, Pallas kernels, local(): pl.pallas_call(kernel, out_shape=(out, out), in_specs=[pl.BlockSpec(memor...  46.5 us
    unnamed x5, local copies, waits for them, and re-layouts  3.41 us

profile of v1, /device:TPU:1, one launch (start us, length us, event | category | flops | bytes accessed | tf_op | source)
XLA Modules:
  0.0 50.6 jit_solution(5926958273015078863)
XLA Ops:
  0.6 1.5 %copy.12.wout_h = f32[128,64]{1,0:T(8,128)} copy(f32[128,64]{0,1:T(8,128)} %param.15) | data formatting | bytes 65536 | tf_op args[5]
  2.1 46.5 %shard_map.113 = (f32[8,512]{1,0:T(8,128)}, f32[8,512]{1,0:T(8,128)}) custom-call(bf16[8,512]{1,0:T(8,128)(2,1)} %uc_h.1, bf16[8,1024]{1,0:T(8,128)(2,1)} %it_h.1, bf16[1024,512]{1,0:T(8,128)(2,1)} %ip_h.1, f32[64,128]{1,0:T(8,128)} %win_h.1, f32[1,128]{1,0:T(1,128)} %bitcast.8, f32[128,64]{1,0:T(8,128)} %copy.12.wout_h, f32[1,64]{1,0:T(1,128)} %bitcast.9, ...), custom_call_target="tpu_custom_call" | custom-call | tf_op jit(solution)/shard_map/pallas_call | solution.py:385
  48.7 0.0 copy-start
  48.7 1.3 %copy.15 = f32[8,512]{1,0:T(8,128)} copy(f32[8,512]{1,0:T(8,128)} %get-tuple-element.4) | data formatting | bytes 32768
  50.0 0.0 copy-done
  50.0 0.6 %copy.16 = f32[8,512]{1,0:T(8,128)} copy(f32[8,512]{1,0:T(8,128)S(1)} %copy-done) | data formatting | bytes 32768
Async XLA Ops:
  48.7 1.3 %copy-start = (f32[8,512]{1,0:T(8,128)S(1)}, f32[8,512]{1,0:T(8,128)}, u32[]{:S(2)}) copy-start(f32[8,512]{1,0:T(8,128)} %get-tuple-element.5) | copy-start | bytes 49156

commit v2 on v1

v2 whole, which is shorter than its diff:
```python
import math

import jax
import jax.numpy as jnp
from jax import lax
from jax.experimental import pallas as pl
from jax.experimental.pallas import tpu as pltpu
from jax.sharding import PartitionSpec as P

MESH = pl.DeviceIdType.MESH
BF16 = jnp.bfloat16
F32 = jnp.float32

COMPS = 8
CDIM = 64
WIDE = COMPS * CDIM
GATES = 64
HIDDEN = 128
ROWS = 8
N_USER = 32
N_ITEM = 16
N_Z = 4
N_Y = 4
N_CORE = 2
N_YC = N_Y * N_CORE
N_X = 4
N_ZL = 4
HALF = COMPS // 2
SPAN = HALF * CDIM
PIECES = 4
PIECE = 1024 // PIECES
USERS = ROWS * N_ITEM
ITEMS = ROWS * N_USER
PAIRS = 1024
LANES = 128
CHUNKS = PAIRS // LANES
LOSS_SCALE = 2.0 * math.sqrt(USERS / (PAIRS * N_ITEM))
NT = (((1,), (1,)), ((), ()))
TN = (((0,), (0,)), ((), ()))


def dot(a, b, dims=(((1,), (0,)), ((), ()))):
    return lax.dot_general(a, b, dims, preferred_element_type=F32)


def split(x):
    upper = x.astype(BF16)
    return upper, (x - upper.astype(F32)).astype(BF16)


def store_parts(ref, x, lanes):
    n = x.shape[0]
    upper, lower = split(x)
    ref[0:n, lanes] = upper
    ref[n : 2 * n, lanes] = lower
    ref[2 * n : 3 * n, lanes] = upper


def chunk(g):
    return slice(g * LANES, (g + 1) * LANES)


def moving(g):
    return pl.ds(pl.multiple_of(g * LANES, LANES), LANES)


def kernel(
    uc_h, it_h, ip_h, win_h, bin_h, wout_h, bout_h, pu_h, pi_h, te_h,
    both_o,
    uc, it, ip, win, bin_, wout, bout, pu, pi, te,
    ubuf, ibuf, bot, bcol, bocol, w1, w2, w3, w4,
    ohu, ohi, up, un, vn, logits, x1, x2, x3, x4, pre_r, sil_r, raw_r, wt_r, res_r, grad_r,
    igt, ugt, isum, usum, iown, uown, asend, abuf, bsend, bbuf, csend, cbuf, dsend, dbuf,
    in_sem, zs, ys, us, isem, usem, as_, asem, bs, bsem, cs, csem, ds_, dsem,
):
    me_u = lax.axis_index("user")
    me_i = lax.axis_index("item")
    z, yc = me_u // N_YC, me_u % N_YC
    y, core = yc // N_CORE, yc % N_CORE
    x, zl = me_i // N_ZL, me_i % N_ZL

    group = [
        (y + dy) % N_Y * N_CORE + (core + dc) % N_CORE
        for dy in (2, 1, 3, 0) for dc in range(N_CORE) if dy or dc
    ]
    z_right, z_left, z_far = ((z + o) % N_Z for o in (1, 3, 2))
    zl_peers = [(zl + o) % N_ZL for o in range(1, N_ZL)]
    x_peers = [(x + o) % N_X for o in (2, 1, 3)]

    pieces = [(ip_h.at[pl.ds(n * PIECE, PIECE)], ip.at[pl.ds(n * PIECE, PIECE)]) for n in range(PIECES)]
    pairs_in = [(it_h, it)] + pieces + [
        (uc_h, uc), (win_h, win), (bin_h, bin_), (wout_h, wout),
        (bout_h, bout), (pu_h, pu), (pi_h, pi), (te_h, te),
    ]
    loads = [pltpu.make_async_copy(s, d, in_sem.at[n]) for n, (s, d) in enumerate(pairs_in)]
    for load in loads:
        load.start()

    barrier = pltpu.get_barrier_semaphore()

    def greet(a, b):
        pl.semaphore_signal(barrier, inc=1, device_id=(a, b), device_id_type=MESH)

    for a in (z_right, z_left):
        greet(a * N_YC + yc, me_i)
    for a in group:
        greet(z * N_YC + a, me_i)
    for b in zl_peers:
        greet(me_u, x * N_ZL + b)
    for b in x_peers:
        greet(me_u, b * N_ZL + zl)

    row = lax.broadcasted_iota(jnp.int32, (WIDE, WIDE), 0)
    col = lax.broadcasted_iota(jnp.int32, (WIDE, WIDE), 1)
    blocks = jnp.where(row // CDIM == col // CDIM, 1.0, 0.0).astype(BF16)
    loads[0].wait()
    mixed = None
    for n in range(PIECES):
        loads[1 + n].wait()
        part = dot(it[:, n * PIECE : (n + 1) * PIECE], ip[n * PIECE : (n + 1) * PIECE, :])
        mixed = part if mixed is None else mixed + part
    upper, lower = split(mixed * mixed)
    square = dot(upper, blocks) + dot(lower, blocks)
    own_item = mixed * lax.rsqrt(square * (1.0 / CDIM) + 1e-06)
    ibuf[me_u] = own_item.astype(BF16)
    loads[1 + PIECES].wait()
    ubuf[me_i] = uc[...]

    pl.semaphore_wait(barrier, 2 + (N_YC - 1) + (N_ZL - 1) + (N_X - 1))

    sends = []

    def send(src, dst, send_sem, recv_sem, a, b):
        copy = pltpu.make_async_remote_copy(
            src_ref=src, dst_ref=dst, send_sem=send_sem, recv_sem=recv_sem,
            device_id=(a, b), device_id_type=MESH,
        )
        copy.start()
        sends.append(copy)

    def arrived(dst, recv_sem):
        pltpu.make_async_remote_copy(
            src_ref=dst, dst_ref=dst, send_sem=zs.at[0], recv_sem=recv_sem,
            device_id=(me_u, me_i), device_id_type=MESH,
        ).wait_recv()

    def item_send(slot, peer, sem):
        send(ibuf.at[slot], ibuf.at[slot], sem, isem.at[slot], peer, me_i)

    def item_arrived(slot):
        arrived(ibuf.at[slot], isem.at[slot])

    def pass_on(source, n):
        for q, a in enumerate(group):
            item_send(source * N_YC + yc, z * N_YC + a, ys.at[n * N_YC + q])

    def user_send(slot, peer, sem):
        send(ubuf.at[slot], ubuf.at[slot], sem, usem.at[slot], me_u, peer)

    def user_arrived(slot):
        arrived(ubuf.at[slot], usem.at[slot])

    item_send(me_u, z_right * N_YC + yc, zs.at[0])
    item_send(me_u, z_left * N_YC + yc, zs.at[1])
    for n, b in enumerate(zl_peers):
        user_send(me_i, x * N_ZL + b, us.at[n])
    pass_on(z, 0)

    def user_pass_on(slot, n):
        for q, b in enumerate(x_peers):
            user_send(slot, b * N_ZL + zl, us.at[n * N_X + q])

    user_pass_on(me_i, 1)

    item_arrived(z_left * N_YC + yc)
    item_send(z_left * N_YC + yc, z_right * N_YC + yc, zs.at[2])
    pass_on(z_left, 1)
    for n, b in enumerate(zl_peers):
        user_arrived(x * N_ZL + b)
        user_pass_on(x * N_ZL + b, 2 + n)
    item_arrived(z_right * N_YC + yc)
    pass_on(z_right, 2)

    for load in loads[2 + PIECES :]:
        load.wait()
    bot[...] = jnp.transpose(jnp.broadcast_to(bout[...], (LANES, GATES)))
    bcol[...] = jnp.transpose(jnp.broadcast_to(bin_[...], (LANES, HIDDEN)))

    def reordered(ref):
        return jnp.concatenate([ref[pl.ds(k, COMPS, stride=COMPS), :] for k in range(COMPS)], axis=0)

    bocol[...] = reordered(bot)
    zeros = jnp.zeros((GATES, HIDDEN), F32)
    for source, tall, flat in ((win, w1, w4), (wout, w3, w2)):
        w = reordered(source)
        upper, lower = split(w)
        flat[:, 0:HIDDEN] = upper
        flat[:, HIDDEN : 2 * HIDDEN] = upper
        flat[:, 2 * HIDDEN : 3 * HIDDEN] = lower
        upper, lower = upper.astype(F32), lower.astype(F32)
        stacked = jnp.concatenate([upper, upper, lower, zeros], axis=0)
        tall[...] = jnp.transpose(stacked).astype(BF16)

    user_range = lax.broadcasted_iota(jnp.int32, (USERS, LANES), 0)
    item_range = lax.broadcasted_iota(jnp.int32, (ITEMS, LANES), 0)
    for g in range(CHUNKS):
        ohu[:, chunk(g)] = jnp.where(user_range == pu[g : g + 1, :], 1.0, 0.0).astype(BF16)
        ohi[:, chunk(g)] = jnp.where(item_range == pi[g : g + 1, :], 1.0, 0.0).astype(BF16)
    x1[3 * GATES :, :] = jnp.zeros((GATES, PAIRS), BF16)
    x3[3 * GATES :, :] = jnp.zeros((GATES, PAIRS), BF16)
    shuffle = jnp.where(col == row % CDIM * COMPS + row // CDIM, 1.0, 0.0).astype(BF16)

    item_arrived(z_far * N_YC + yc)
    pass_on(z_far, 3)

    for a in x_peers:
        for b in range(N_ZL):
            user_arrived(a * N_ZL + b)
    user_tile = ubuf[...].astype(F32).reshape(USERS, WIDE).astype(BF16)
    un[...] = dot(user_tile, ohu[...], TN)
    up[...] = dot(dot(user_tile, shuffle).astype(BF16), ohu[...], TN)

    for a in (z, z_left, z_right, z_far):
        for b in group:
            item_arrived(a * N_YC + b)
    item_tile = ibuf[...].astype(F32).reshape(ITEMS, WIDE).astype(BF16)
    vn[...] = dot(item_tile, ohi[...], TN).reshape(vn.shape)

    def logit_chunk(g, _):
        lanes = moving(g)

        total = [jnp.zeros((COMPS, LANES), F32)] * COMPS
        for d in range(CDIM):
            u = up[d * COMPS : (d + 1) * COMPS, lanes]
            for k in range(COMPS):
                total[k] = total[k] + u * vn[k * 8 + d // 8, d % 8 : d % 8 + 1, lanes]
        flat = jnp.concatenate(total, axis=0) * (1.0 / math.sqrt(CDIM))
        logits[:, lanes] = flat
        store_parts(x1, flat, lanes)
        return 0

    lax.fori_loop(0, CHUNKS, logit_chunk, 0)

    pre_r[...] = dot(w1[...], x1[...])
    for g in range(CHUNKS):
        pre = pre_r[:, chunk(g)] + bcol[...]
        sig = 0.5 * jnp.tanh(0.5 * pre) + 0.5
        store_parts(x2, pre * sig, chunk(g))
        sil_r[:, chunk(g)] = sig * (1.0 + pre * (1.0 - sig))
    raw_r[...] = dot(w2[...], x2[...])
    for g in range(CHUNKS):
        capped = jnp.tanh((raw_r[:, chunk(g)] + bocol[...]) * 0.125)
        powers = jnp.exp(8.0 * capped)
        weights = powers * (1.0 / jnp.sum(powers, axis=0, keepdims=True))
        flat = logits[:, chunk(g)]
        student = jnp.sum(weights * flat, axis=0, keepdims=True)
        store_parts(x3, weights * (flat - student) * (1.0 - capped * capped), chunk(g))
        wt_r[:, chunk(g)] = weights
        res_r[g : g + 1, :] = (student - te[g : g + 1, :]) * LOSS_SCALE
    pre_r[...] = dot(w3[...], x3[...])
    for g in range(CHUNKS):
        store_parts(x4, pre_r[:, chunk(g)] * sil_r[:, chunk(g)], chunk(g))
    raw_r[...] = dot(w4[...], x4[...])
    for g in range(CHUNKS):
        d_flat = res_r[g : g + 1, :] * (wt_r[:, chunk(g)] + raw_r[:, chunk(g)])
        grad_r[:, chunk(g)] = (d_flat * (1.0 / math.sqrt(CDIM))).astype(BF16).astype(F32)

    def expand(out, base, pick, values):
        def step(g, _):
            lanes = moving(g)
            factors = [
                [jnp.broadcast_to(grad_r[pick(i, j) : pick(i, j) + 1, lanes], (8, LANES)) for i in range(COMPS)]
                for j in range(HALF)
            ]
            for block in range(0, 8, 2):
                sums = [[], []]
                for n in range(2):
                    terms = [values(i, block + n, lanes) for i in range(COMPS)]
                    for j in range(HALF):
                        products = [f * t for f, t in zip(factors[j], terms)]
                        while len(products) > 1:
                            products = [a + b for a, b in zip(products[::2], products[1::2])]
                        sums[n].append(products[0])
                for j in range(HALF):
                    start = base + j * CDIM + block * 8
                    out[start : start + 16, lanes] = jnp.concatenate([sums[0][j], sums[1][j]], axis=0).astype(BF16)
            return 0

        lax.fori_loop(0, CHUNKS, step, 0)

    def item_values(c, block, lanes):
        return un[c * CDIM + block * 8 : c * CDIM + block * 8 + 8, lanes]

    for h in range(2):
        expand(igt, h * SPAN, lambda c, j: (h * HALF + j) * COMPS + c, item_values)
        part = dot(ohi[...], igt[h * SPAN : (h + 1) * SPAN, :], NT).reshape(N_Z, N_YC, ROWS, SPAN)
        isum[h] = part
        asend[h] = part.astype(BF16)
        for q, a in enumerate(group):
            send(
                asend.at[h, :, a], abuf.at[h, yc], as_.at[h * N_YC + q], asem.at[h * N_YC + yc],
                z * N_YC + a, me_i,
            )

    def user_values(k, block, lanes):
        return vn[k * 8 + block, :, lanes]

    for h in range(2):
        expand(ugt, h * SPAN, lambda k, j: k * COMPS + h * HALF + j, user_values)
    usum[...] = dot(ohu[...], ugt[...], NT).reshape(N_X, N_ZL, ROWS, WIDE)
    csend[...] = usum[...].astype(BF16)
    for q, b in enumerate(x_peers):
        send(csend.at[b], cbuf.at[x], cs.at[q], csem.at[x], me_u, b * N_ZL + zl)

    for h in range(2):
        total = isum[h, :, yc]
        for a in group[::-1]:
            arrived(abuf.at[h, a], asem.at[h * N_YC + a])
            total = total + abuf[h, a].astype(F32)
        bsend[h] = total.astype(BF16)
        iown[h] = total
        for q, a in enumerate((z_far, z_right, z_left)):
            send(
                bsend.at[h, a], bbuf.at[h, z], bs.at[h * N_Z + q], bsem.at[h * N_Z + z],
                a * N_YC + yc, me_i,
            )

    total = usum[x]
    for b in x_peers[::-1]:
        arrived(cbuf.at[b], csem.at[b])
        total = total + cbuf[b].astype(F32)
    dsend[...] = total.astype(BF16)
    uown[...] = total
    for q, b in enumerate(zl_peers):
        send(dsend.at[b], dbuf.at[zl], ds_.at[q], dsem.at[zl], me_u, x * N_ZL + b)
    total = uown[zl]
    for b in zl_peers:
        arrived(dbuf.at[b], dsem.at[b])
        total = total + dbuf[b].astype(F32)
    both_o[0] = total

    for h in range(2):
        total = iown[h, z]
        for a in (z_right, z_left, z_far):
            arrived(bbuf.at[h, a], bsem.at[h * N_Z + a])
            total = total + bbuf[h, a].astype(F32)
        both_o[1, :, h * SPAN : (h + 1) * SPAN] = total

    for copy in sends:
        copy.wait_send()


def local(
    user_comps, item_text, item_proj, w_in, b_in, w_out, b_out, pair_user, pair_item, teacher
):
    def vmem(shape, kind=F32):
        return pltpu.VMEM(shape, kind)

    inputs = (
        user_comps, item_text, item_proj, w_in, b_in.reshape(1, -1), w_out.T, b_out.reshape(1, -1),
        pair_user.reshape(CHUNKS, LANES), pair_item.reshape(CHUNKS, LANES), teacher.reshape(CHUNKS, LANES),
    )
    dma = pltpu.SemaphoreType.DMA
    scratch = [vmem(a.shape, a.dtype) for a in inputs] + [
        vmem((N_ITEM, ROWS, WIDE), BF16),
        vmem((N_USER, ROWS, WIDE), BF16),
        vmem((GATES, LANES)),
        vmem((HIDDEN, LANES)),
        vmem((GATES, LANES)),
        vmem((HIDDEN, 4 * GATES), BF16),
        vmem((GATES, 3 * HIDDEN), BF16),
        vmem((HIDDEN, 4 * GATES), BF16),
        vmem((GATES, 3 * HIDDEN), BF16),
        vmem((USERS, PAIRS), BF16),
        vmem((ITEMS, PAIRS), BF16),
        vmem((WIDE, PAIRS)),
        vmem((WIDE, PAIRS)),
        vmem((WIDE // 8, 8, PAIRS)),
        vmem((GATES, PAIRS)),
        vmem((4 * GATES, PAIRS), BF16),
        vmem((3 * HIDDEN, PAIRS), BF16),
        vmem((4 * GATES, PAIRS), BF16),
        vmem((3 * HIDDEN, PAIRS), BF16),
        vmem((HIDDEN, PAIRS)),
        vmem((HIDDEN, PAIRS)),
        vmem((GATES, PAIRS)),
        vmem((GATES, PAIRS)),
        vmem((CHUNKS, LANES)),
        vmem((GATES, PAIRS)),
        vmem((WIDE, PAIRS), BF16),
        vmem((WIDE, PAIRS), BF16),
        vmem((2, N_Z, N_YC, ROWS, SPAN)),
        vmem((N_X, N_ZL, ROWS, WIDE)),
        vmem((2, N_Z, ROWS, SPAN)),
        vmem((N_ZL, ROWS, WIDE)),
        vmem((2, N_Z, N_YC, ROWS, SPAN), BF16),
        vmem((2, N_YC, N_Z, ROWS, SPAN), BF16),
        vmem((2, N_Z, ROWS, SPAN), BF16),
        vmem((2, N_Z, ROWS, SPAN), BF16),
        vmem((N_X, N_ZL, ROWS, WIDE), BF16),
        vmem((N_X, N_ZL, ROWS, WIDE), BF16),
        vmem((N_ZL, ROWS, WIDE), BF16),
        vmem((N_ZL, ROWS, WIDE), BF16),
        dma((len(inputs) - 1 + PIECES,)),
        dma((N_Z,)),
        dma((N_Z * N_YC,)),
        dma(((N_ZL + 1) * N_X,)),
        dma((N_USER,)),
        dma((N_ITEM,)),
        dma((2 * N_YC,)),
        dma((2 * N_YC,)),
        dma((2 * N_Z,)),
        dma((2 * N_Z,)),
        dma((N_X,)),
        dma((N_X,)),
        dma((N_ZL,)),
        dma((N_ZL,)),
    ]
    both = pl.pallas_call(
        kernel,
        out_shape=pltpu.VMEM((2, ROWS, WIDE), F32),
        in_specs=[pl.BlockSpec(memory_space=pl.ANY)] * len(inputs),
        out_specs=pl.BlockSpec(memory_space=pltpu.VMEM),
        scratch_shapes=scratch,
        compiler_params=pltpu.CompilerParams(
            collective_id=0, has_side_effects=True, vmem_limit_bytes=60 * 1024 * 1024
        ),
    )(*inputs)
    return both[0], both[1]


def solution(mesh):
    split_both = P(("user", "item"), None)
    split_one = P(("user", "item"))
    in_specs = (
        split_both, split_both, P(), P(), P(), P(), P(), split_one, split_one, split_one,
    )
    return jax.shard_map(
        local, mesh=mesh, in_specs=in_specs, out_specs=(split_both, split_both), check_vma=False
    )
```

time: 50.9 us -> 45.4 us (0.89)
  local copies, waits for them, and re-layouts: 3.41 us -> 0.61 us
  Pallas kernels: 46.5 us -> 44 us
    unnamed x5 -> x0, local copies, waits for them, and re-layouts: 3.41 us -> none
    pallas_call x1, Pallas kernels: 46.5 us -> 44 us  [local(): pl.pallas_call(kernel, out_shape=pltpu.VMEM((2, ROWS, WIDE), F32), in_spe...]
    squeeze x0 -> x1, local copies, waits for them, and re-layouts: none -> 0.61 us  [local(): return (both[0], both[1])]
where the time goes in v2:
time: 45.4 us; the launch traced here: 45.3 us
  Pallas kernels  44 us (97%)
  between operations  0.64 us (1%)
  local copies, waits for them, and re-layouts  0.61 us (1%)
    pallas_call x1, Pallas kernels, local(): pl.pallas_call(kernel, out_shape=pltpu.VMEM((2, ROWS, WIDE), F32), in_spe...  44 us

profile of v2, /device:TPU:1, one launch (start us, length us, event | category | flops | bytes accessed | tf_op | source)
XLA Modules:
  0.0 45.3 jit_solution(12094047256402760541)
XLA Ops:
  0.6 44.0 %shard_map.113 = f32[2,8,512]{2,1,0:T(8,128)S(1)} custom-call(bf16[8,512]{1,0:T(8,128)(2,1)} %uc_h.1, bf16[8,1024]{1,0:T(8,128)(2,1)} %it_h.1, bf16[1024,512]{1,0:T(8,128)(2,1)} %ip_h.1, f32[64,128]{1,0:T(8,128)} %win_h.1, f32[1,128]{1,0:T(1,128)} %bitcast.14, f32[64,128]{1,0:T(8,128)} %bitcast.10, f32[1,64]{1,0:T(1,128)} %bitcast.15, s32[8,128]{1,0:T(8,128)} %bitcast.11, ...), custom_call_target="tpu_custom_call" | custom-call | tf_op jit(solution)/shard_map/pallas_call | solution.py:419
  44.7 0.6 %slice_bitcast_fusion = (f32[8,512]{1,0:T(8,128)}, f32[8,512]{1,0:T(8,128)}) fusion(f32[2,8,512]{2,1,0:T(8,128)S(1)} %shard_map.113), kind=kLoop, calls=%fused_computation | loop fusion | bytes 65536 | tf_op jit(solution)/shard_map/squeeze | solution.py:429
